TPU v7x, 256 devices: a whole 4x4x8 slice. The times are simulated.
256 devices in a mesh: row: 8 (over y, z_lo), col: 8 (over z_hi, core), layer: 4 (over x).
Axes of the slice: x: 4, y: 4, z: 8 (z_hi: 4, z_lo: 2; z = z_hi * 2 + z_lo), core: 2. Of those that a mesh axis runs over, the one named last changes fastest.
Arguments:
- density_tiles: bfloat16 [192, 8, 2, 128, 128], P(('row', 'col')), may hold values from -1.5 to 1.5
- tile_columns: int32 [192, 8, 2], P(('row', 'col')), may hold values from -1 to 191, as said below
Outputs:
- square_tiles: bfloat16 [192, 8, 2, 128, 128], P(('row', 'col'), None, None, 'layer')
Inputs may be any that keep to these rules, and one draw needn't show every extreme that they name: `tile_columns`: entry [i, g, s] is a tile column in group g (columns g * 24 to (g + 1) * 24 - 1) or -1; within one block row and group the listed columns are distinct and empty slots come after the listed ones; block row i lists its own column i in the first slot of its group, whose 2 slots are all listed; other groups hold 0 to 2 listed tiles.
All inputs are finite; a program needn't handle non-finite values.
Results may differ from a plain program's by a relative error of at most 0.0048.
Values may be sent and summed in bfloat16 or wider, within the bound.
No kernel may reach another device: no remote copies, remote signals or barrier semaphores. Data moves between devices by JAX's collectives and lax.ppermute only.
A program may use at most 64 MiB of HBM per device.

v0:
```python
import jax
import jax.numpy as jnp
from jax import lax
from jax.sharding import Mesh
from jax.sharding import PartitionSpec as P

ROW = ("row_0", "row_1")
ROW_COL = ("row_0", "row_1", "col")


def filled_up(lines, devices):
    spare = -len(lines) % devices
    return jnp.pad(lines, [(0, spare)] + [(0, 0)] * (lines.ndim - 1))


def spread(array, axis, root):
    lines = jnp.where(lax.axis_index(axis) == root, array, jnp.zeros_like(array)).reshape(
        -1, *array.shape[1:][-1:]
    )
    padded = filled_up(lines, lax.axis_size(axis))
    own = lax.psum_scatter(padded, axis, scatter_dimension=0, tiled=True)
    return lax.all_gather(own, axis, axis=0, tiled=True)[: len(lines)].reshape(array.shape)


def broadcast_by_axis(array, axes, root):
    array = jnp.where(lax.axis_index(axes) == root, array, jnp.zeros_like(array))
    for axis in axes:
        array = lax.psum(array, axis)
    return array


def in_blocks(array, dim, devices):
    before, after = (array.shape[:dim], array.shape[dim + 1 :])
    return jnp.moveaxis(array.reshape(*before, devices, -1, *after), dim, 0)


def sent_and_summed(array, axis, dim):
    pieces = in_blocks(array, dim, lax.axis_size(axis))
    arrived = lax.all_to_all(pieces, axis, split_axis=0, concat_axis=0, tiled=True)
    return arrived.astype(jnp.float32).sum(axis=0)


def multiply(left_tiles, left_columns, right_tiles, right_columns, target_columns, start_row):
    is_live = left_columns >= 0
    inner_rows = jnp.where(is_live, left_columns - start_row, 0).astype(jnp.int32)
    inner_columns = right_columns[inner_rows]
    matches = (
        (inner_columns[:, :, None, :] == target_columns[:, None, :, None])
        & is_live[:, :, None, None]
        & (target_columns >= 0)[:, None, :, None]
    )
    slot_index = jnp.argmax(matches.astype(jnp.int32), axis=-1)
    located = jnp.any(matches, axis=-1)
    selected = right_tiles[inner_rows[:, :, None], slot_index]
    selected = jnp.where(located[:, :, :, None, None], selected, jnp.zeros((), jnp.bfloat16))
    return jnp.einsum("iarc,iascd->isrd", left_tiles, selected, preferred_element_type=jnp.float32)


def on_device(density_tiles, tile_columns):
    row_count = lax.axis_size(ROW)
    column_count = lax.axis_size("col")
    layer_count = lax.axis_size("layer")
    grid_tiles, grid_columns = (
        lax.all_to_all(density_tiles, "col", split_axis=1, concat_axis=0, tiled=True),
        lax.all_to_all(tile_columns, "col", split_axis=1, concat_axis=0, tiled=True),
    )
    block_tiles = grid_tiles[:, 0]
    block_columns = grid_columns[:, 0]
    group_rows = block_tiles.shape[0]
    row_ratio = column_count // row_count
    panel_rows = group_rows // row_ratio
    per_layer = column_count // layer_count
    layer_index = lax.axis_index("layer")
    partial_value = jnp.zeros(block_tiles.shape, jnp.float32)
    for panel_step in range(per_layer):
        panel_index = layer_index * per_layer + panel_step
        left_tiles, left_columns = (
            spread(block_tiles, "col", panel_index),
            spread(block_columns, "col", panel_index),
        )
        right_tiles, right_columns = (
            broadcast_by_axis(block_tiles, ROW, panel_index // row_ratio),
            broadcast_by_axis(block_columns, ROW, panel_index // row_ratio),
        )
        partial_value = partial_value + multiply(
            left_tiles,
            left_columns,
            right_tiles,
            right_columns,
            block_columns,
            panel_index * panel_rows,
        )
    rounded = partial_value.astype(jnp.bfloat16)
    summed = sent_and_summed(rounded.astype(jnp.float32).astype(jnp.bfloat16), "layer", 2)
    returned = lax.all_to_all(
        summed.astype(jnp.bfloat16)[:, None], "col", split_axis=0, concat_axis=1, tiled=True
    )
    return returned


def solution(mesh):
    split = Mesh(
        mesh.devices.reshape(4, 2, mesh.shape["col"], mesh.shape["layer"]),
        ("row_0", "row_1", "col", "layer"),
    )
    return jax.shard_map(
        on_device,
        mesh=split,
        in_specs=(P(ROW_COL, None, None, None, None), P(ROW_COL, None, None)),
        out_specs=P(ROW_COL, None, None, "layer", None),
        check_vma=False,
    )
```

profile of v0, /device:TPU:1, one launch (start us, length us, event | category | flops | bytes accessed | tf_op | source)
XLA Modules:
  0.0 319.0 jit_solution(11141987187466286460)
XLA Ops:
  7.4 2.7 copy.204
  10.1 10.0 %all-to-all-start.1 = ((bf16[3,8,2,128,128]{4,3,2,0,1:T(8,128)(2,1)}), bf16[3,8,2,128,128]{4,3,2,0,1:T(8,128)(2,1)S(1)}, u32[]{:S(2)}, u32[]{:S(2)}) async-start(bf16[3,8,2,128,128]{4,3,2,0,1:T(8,128)(2,1)} %copy.204), calls=%async_computation.1 | async-start | bytes 3145728 | tf_op jit(solution)/shard_map/all_to_all | solution.py:64
  20.1 33.3 %all-to-all-done.1 = bf16[3,8,2,128,128]{4,3,2,0,1:T(8,128)(2,1)S(1)} async-done(((bf16[3,8,2,128,128]{4,3,2,0,1:T(8,128)(2,1)}), bf16[3,8,2,128,128]{4,3,2,0,1:T(8,128)(2,1)S(1)}, u32[]{:S(2)}, u32[]{:S(2)}) %all-to-all-start.1) | async-done | bytes 1572896 | tf_op jit(solution)/shard_map/all_to_all | solution.py:64
  53.4 2.8 broadcast_select_fusion.2
  56.3 0.5 reduce-scatter.5.cloned.1.call-update
  56.8 0.5 reduce-scatter.3.cloned.1.call-update
  57.4 82.9 %all-reduce.10.cloned.1.call-done = (bf16[24,2,128,128]{3,2,1,0:T(8,128)(2,1)}, bf16[24,2,128,128]{3,2,1,0:T(8,128)(2,1)}) async-done(((bf16[24,2,128,128]{3,2,1,0:T(8,128)(2,1)}, bf16[24,2,128,128]{3,2,1,0:T(8,128)(2,1)}), (bf16[24,2,128,128]{3,2,1,0:T(8,128)(2,1)}, bf16[24,2,128,128]{3,2,1,0:T(8,128)(2,1)})) %all-reduce.10.cloned.1.call-update) | async-done | bytes 3145744 | tf_op jit(solution)/shard_map/psum | solution.py:28
  140.4 0.5 all-gather.7.cloned.1.call-update
  141.0 0.7 copy.187
  141.7 7.8 %all-to-all-start = ((s32[3,8,2]{0,2,1:T(2,128)}), s32[3,8,2]{0,2,1:T(2,128)S(1)}, u32[]{:S(2)}, u32[]{:S(2)}) async-start(s32[3,8,2]{0,2,1:T(2,128)} %copy.187), calls=%async_computation | async-start | bytes 16384 | tf_op jit(solution)/shard_map/all_to_all | solution.py:65
  149.5 0.6 dynamic-slice
  150.7 5.9 %all-to-all-done = s32[3,8,2]{0,2,1:T(2,128)S(1)} async-done(((s32[3,8,2]{0,2,1:T(2,128)}), s32[3,8,2]{0,2,1:T(2,128)S(1)}, u32[]{:S(2)}, u32[]{:S(2)}) %all-to-all-start) | async-done | bytes 224 | tf_op jit(solution)/shard_map/all_to_all | solution.py:65
  156.8 25.1 %all-reduce.2 = (s32[24,2]{1,0:T(8,128)S(1)}, s32[24,2]{1,0:T(8,128)S(1)}) all-reduce(s32[24,2]{1,0:T(8,128)S(1)} %get-tuple-element.32, s32[24,2]{1,0:T(8,128)S(1)} %get-tuple-element.34), channel_id=4, replica_groups=mesh['row_0'=4,'row_1'=2,'col'=8,'layer'=4] {'col'}, use_global_device_ids=true, to_apply=%region_10.11.clone | all-reduce | flops 96 | bytes 768
  181.9 0.1 copy.192
  182.0 12.9 %all-gather = s32[8,3,2]{1,2,0:T(2,128)S(1)} all-gather(s32[1,3,2]{1,2,0:T(2,128)S(1)} %bitcast.110), channel_id=1, replica_groups=mesh['row_0'=4,'row_1'=2,'col'=8,'layer'=4] {'col'}, dimensions={0}, use_global_device_ids=true | all-gather | bytes 216 | tf_op jit(solution)/shard_map/all_gather | solution.py:22
  195.1 0.1 copy.202
  195.2 0.1 copy.210
  195.3 0.1 copy.194
  195.5 0.1 copy.197
  195.7 13.0 %all-gather.1 = s32[8,3,2]{1,2,0:T(2,128)S(1)} all-gather(s32[1,3,2]{1,2,0:T(2,128)S(1)} %bitcast.109), channel_id=1, replica_groups=mesh['row_0'=4,'row_1'=2,'col'=8,'layer'=4] {'col'}, dimensions={0}, use_global_device_ids=true | all-gather | bytes 216 | tf_op jit(solution)/shard_map/all_gather | solution.py:22
  208.8 0.1 copy.212
  209.0 0.1 copy.215
  209.5 0.1 reshape.81
  209.6 13.5 %all-reduce.3 = (s32[24,2]{1,0:T(8,128)S(1)}, s32[24,2]{1,0:T(8,128)S(1)}) all-reduce(s32[24,2]{1,0:T(8,128)S(1)} %get-tuple-element.33, s32[24,2]{1,0:T(8,128)S(1)} %get-tuple-element.31), channel_id=1, replica_groups=mesh['row_0'=4,'row_1'=2,'col'=8,'layer'=4] {'row_0'}, use_global_device_ids=true, to_apply=%region_8.9 | all-reduce | flops 96 | bytes 768 | tf_op jit(solution)/shard_map/psum | solution.py:28
  223.0 7.7 %all-reduce.4 = (s32[24,2]{1,0:T(8,128)S(1)}, s32[24,2]{1,0:T(8,128)S(1)}) all-reduce(s32[24,2]{1,0:T(8,128)S(1)} %get-tuple-element.11, s32[24,2]{1,0:T(8,128)S(1)} %get-tuple-element.12), channel_id=1, replica_groups=mesh['row_0'=4,'row_1'=2,'col'=8,'layer'=4] {'row_1'}, use_global_device_ids=true, to_apply=%region_9.10 | all-reduce | flops 96 | bytes 768 | tf_op jit(solution)/shard_map/psum | solution.py:28
  230.7 0.6 gather_fusion.2
  231.3 0.1 copy.218
  231.6 0.1 reshape.67
  231.7 0.6 gather_fusion
  232.4 0.1 copy.203
  232.5 0.1 copy.219
  232.7 0.6 iota_reduce_fusion
  233.3 0.1 copy.221
  233.4 0.1 reshape.87
  233.5 0.6 iota_reduce_fusion.1
  234.2 0.1 copy.206
  234.3 0.1 reshape.73
  234.4 11.8 %all-reduce.12.cloned.1.call-done = (bf16[24,2,128,128]{3,2,1,0:T(8,128)(2,1)}, bf16[24,2,128,128]{3,2,1,0:T(8,128)(2,1)}) async-done(((bf16[24,2,128,128]{3,2,1,0:T(8,128)(2,1)}, bf16[24,2,128,128]{3,2,1,0:T(8,128)(2,1)}), (bf16[24,2,128,128]{3,2,1,0:T(8,128)(2,1)}, bf16[24,2,128,128]{3,2,1,0:T(8,128)(2,1)})) %all-reduce.12.cloned.1.call-update) | async-done | bytes 3145744 | tf_op jit(solution)/shard_map/psum | solution.py:28
  246.2 4.5 %gather_fusion.3 = bf16[96,128,128]{2,1,0:T(8,128)(2,1)} fusion(bf16[24,2,128,128]{3,2,1,0:T(8,128)(2,1)} %get-tuple-element.17, s32[96]{0:T(128)S(1)} %reshape.87), kind=kCustom, calls=%fused_computation.3 | custom fusion | bytes 6292224 | tf_op jit(solution)/shard_map/gather | solution.py:54
  250.6 3.0 gather_fusion.1
  253.7 4.8 %fusion.1 = f32[24,2,128,128,1]{2,3,1,4,0:T(8,128)} fusion(bf16[24,2,128,128,1]{3,2,4,1,0:T(8,128)(2,1)} %bitcast.105, bf16[24,2,2,128,128]{4,3,2,1,0:T(8,128)(2,1)} %bitcast.95, pred[24,2,2]{2,1,0:T(4,128)(4,1)S(1)} %copy.219), kind=kOutput, calls=%fused_computation.6 | convolution fusion | flops 404226048 | bytes 7864416 | tf_op jit(solution)/shard_map/iarc,iascd->isrd/dot_general | solution.py:56
  258.5 5.5 %all-gather.5.cloned.1.call-done = bf16[6144,128]{1,0:T(8,128)(2,1)} async-done(((bf16[768,128]{1,0:T(8,128)(2,1)}), bf16[6144,128]{1,0:T(8,128)(2,1)}) %all-gather.5.cloned.1.call-update) | async-done | bytes 1572880 | tf_op jit(solution)/shard_map/all_gather | solution.py:22
  263.9 3.0 fusion
  267.0 0.4 copy.235
  267.4 24.0 %all_to_all.47 = bf16[4,24,2,32,128]{4,3,2,1,0:T(8,128)(2,1)S(1)} all-to-all(bf16[4,24,2,32,128]{4,3,2,1,0:T(8,128)(2,1)S(1)} %bitcast.97), channel_id=1, replica_groups=mesh['row_0'=4,'row_1'=2,'col'=8,'layer'=4] {'layer'}, dimensions={0} | all-to-all | bytes 3145728 | tf_op jit(solution)/shard_map/all_to_all | solution.py:39
  291.4 0.3 reduce_sum.12
  291.8 18.9 %all_to_all.48 = bf16[24,1,2,32,128]{4,3,2,1,0:T(8,128)(2,1)S(1)} all-to-all(bf16[24,1,2,32,128]{4,3,2,1,0:T(8,128)(2,1)S(1)} %bitcast.104), channel_id=1, replica_groups=mesh['row_0'=4,'row_1'=2,'col'=8,'layer'=4] {'col'}, dimensions={0} | all-to-all | bytes 786432 | tf_op jit(solution)/shard_map/all_to_all | solution.py:95
  310.6 0.8 copy.224
  (46 shorter events, 1.8 us)
Async XLA Ops:
  10.1 43.3 %all-to-all-start.1 = ((bf16[3,8,2,128,128]{4,3,2,0,1:T(8,128)(2,1)}), bf16[3,8,2,128,128]{4,3,2,0,1:T(8,128)(2,1)S(1)}, u32[]{:S(2)}, u32[]{:S(2)}) async-start(bf16[3,8,2,128,128]{4,3,2,0,1:T(8,128)(2,1)} %copy.204), calls=%async_computation.1 | async-start | bytes 3145728 | tf_op jit(solution)/shard_map/all_to_all | solution.py:64
  20.1 120.3 %all-reduce.10.cloned.1.call-start = ((), (), s32[]{:S(2)}) async-start(), calls=%async_computation.10 | async-start | bytes 6291456 | tf_op jit(solution)/shard_map/psum | solution.py:28
  56.2 84.2 %reduce-scatter.5.cloned.1.call-start = ((), (), s32[]{:S(2)}) async-start(), calls=%async_computation.8 | async-start | bytes 1769472 | tf_op jit(solution)/shard_map/reduce_scatter | solution.py:21
  56.8 138.2 %reduce-scatter.3.cloned.1.call-start = ((), (), s32[]{:S(2)}) async-start(), calls=%async_computation.6 | async-start | bytes 1769472 | tf_op jit(solution)/shard_map/reduce_scatter | solution.py:21
  57.4 188.8 %all-reduce.12.cloned.1.call-start = ((), (), s32[]{:S(2)}) async-start(), calls=%async_computation.11 | async-start | bytes 6291456 | tf_op jit(solution)/shard_map/psum | solution.py:28
  140.3 0.7 copy-start
  140.3 9.2 %copy-start.1 = (u32[256]{0:T(256)S(1)}, u32[256]{0:T(256)}, u32[]{:S(2)}) copy-start(u32[256]{0:T(256)} %constant.100) | copy-start | bytes 3076
  140.3 113.3 %all-gather.7.cloned.1.call-start = ((), (), s32[]{:S(2)}) async-start(), calls=%async_computation.9 | async-start | bytes 1769472 | tf_op jit(solution)/shard_map/all_gather | solution.py:22
  141.7 14.9 %all-to-all-start = ((s32[3,8,2]{0,2,1:T(2,128)}), s32[3,8,2]{0,2,1:T(2,128)S(1)}, u32[]{:S(2)}, u32[]{:S(2)}) async-start(s32[3,8,2]{0,2,1:T(2,128)} %copy.187), calls=%async_computation | async-start | bytes 16384 | tf_op jit(solution)/shard_map/all_to_all | solution.py:65
  149.5 114.4 %all-gather.5.cloned.1.call-start = ((), (), s32[]{:S(2)}) async-start(), calls=%async_computation.7 | async-start | bytes 1769472 | tf_op jit(solution)/shard_map/all_gather | solution.py:22
Sparse Core Ops, SparseCore 0:
  56.3 83.9 all-reduce.9
  143.0 103.1 all-reduce.11
Sparse Core Ops, SparseCore 1:
  59.3 43.9 reduce-scatter.4
  105.7 40.1 reduce-scatter.2
  147.6 63.6 all-gather.6
  213.1 50.8 all-gather.4
where the time goes:
time: 319 us
  waiting for transfers between devices  141 us (44%)
  blocking collectives  115 us (36%)
  starting transfers between devices  18 us (6%)
  local copies, waits for them, and re-layouts  16.9 us (5%)
  between operations  15.8 us (5%)
  matrix products  7.82 us (2%)
  other arithmetic  4.51 us (1%)
    psum x2, waiting for transfers between devices, broadcast_by_axis(): array = lax.psum(array, axis)  94.7 us
    all_to_all x1, waiting for transfers between devices, on_device(): lax.all_to_all(density_tiles, 'col', split_axis=1, concat_axis=0, tiled=T...  33.3 us
    all_gather x2, blocking collectives, spread(): lax.all_gather(own, axis, axis=0, tiled=True)[:len(lines)]  25.9 us
    unnamed x1, blocking collectives  25.1 us
    all_to_all x1, blocking collectives, sent_and_summed(): lax.all_to_all(pieces, axis, split_axis=0, concat_axis=0, tiled=True)  24 us
    psum x2, blocking collectives, broadcast_by_axis(): array = lax.psum(array, axis)  21.2 us
    all_to_all x1, blocking collectives, on_device(): lax.all_to_all(summed.astype(jnp.bfloat16)[:, None], 'col', split_axis=0,...  18.9 us
    all_to_all x1, starting transfers between devices, on_device(): lax.all_to_all(density_tiles, 'col', split_axis=1, concat_axis=0, tiled=T...  9.95 us
  transfers between devices with their start and end apart: 8, of which 5 were waited for; matrix products, arithmetic and copies ran while one was open for 6% of the time, Pallas kernels for 0%

commit v1 on v0

--- a/solution.py
+++ b/solution.py
@@ -25,7 +25,11 @@
 def broadcast_by_axis(array, axes, root):
     array = jnp.where(lax.axis_index(axes) == root, array, jnp.zeros_like(array))
     for axis in axes:
-        array = lax.psum(array, axis)
+
+        def time_kinds(frame_in, a_name):
+            return jnp.sum(lax.all_gather(frame_in, a_name), axis=0)
+
+        array = time_kinds(array, axis)
     return array
 
 

time: 319 us -> 428 us (1.34)
  waiting for transfers between devices: 141 us -> 251 us
  blocking collectives: 115 us -> 96.8 us
  other arithmetic: 4.51 us -> 21.6 us
    all_gather x0 -> x4, waiting for transfers between devices: none -> 155 us  [time_kinds(): return jnp.sum(lax.all_gather(frame_in, a_name), axis=0)]
    psum x2 -> x0, waiting for transfers between devices: 94.7 us -> none  [broadcast_by_axis(): array = lax.psum(array, axis)]
    all_gather x2, waiting for transfers between devices: 5.51 us -> 55 us  [spread(): lax.all_gather(own, axis, axis=0, tiled=True)[:len(lines)]]
    psum x2 -> x0, blocking collectives: 21.2 us -> none  [broadcast_by_axis(): array = lax.psum(array, axis)]
    all_gather x0 -> x4, blocking collectives: none -> 18.7 us  [time_kinds(): return jnp.sum(lax.all_gather(frame_in, a_name), axis=0)]
    unnamed x1, blocking collectives: 25.1 us -> 7.27 us
    reduce_sum x0 -> x8, other arithmetic: none -> 17 us  [time_kinds(): return jnp.sum(lax.all_gather(frame_in, a_name), axis=0)]
  transfers between devices with their start and end apart: 8 -> 10, of which waited for: 5 -> 7; matrix products, arithmetic and copies ran while one was open for 6% -> 8% of each run, Pallas kernels for 0% -> 0%
where the time goes in v1:
time: 428 us; the launch traced here: 427 us
  waiting for transfers between devices  251 us (59%)
  blocking collectives  96.8 us (23%)
  other arithmetic  21.6 us (5%)
  starting transfers between devices  18.1 us (4%)
  local copies, waits for them, and re-layouts  15.7 us (4%)
  between operations  15.7 us (4%)
  matrix products  7.86 us (2%)
    all_gather x4, waiting for transfers between devices, time_kinds(): return jnp.sum(lax.all_gather(frame_in, a_name), axis=0)  155 us
    all_gather x2, waiting for transfers between devices, spread(): lax.all_gather(own, axis, axis=0, tiled=True)[:len(lines)]  55 us
    all_to_all x1, waiting for transfers between devices, on_device(): lax.all_to_all(density_tiles, 'col', split_axis=1, concat_axis=0, tiled=T...  33.3 us
    all_gather x2, blocking collectives, spread(): lax.all_gather(own, axis, axis=0, tiled=True)[:len(lines)]  27.8 us
    all_to_all x1, blocking collectives, sent_and_summed(): lax.all_to_all(pieces, axis, split_axis=0, concat_axis=0, tiled=True)  25.3 us
    all_gather x4, blocking collectives, time_kinds(): return jnp.sum(lax.all_gather(frame_in, a_name), axis=0)  18.7 us
    all_to_all x1, blocking collectives, on_device(): lax.all_to_all(summed.astype(jnp.bfloat16)[:, None], 'col', split_axis=0,...  17.7 us
    reduce_sum x8, other arithmetic, time_kinds(): return jnp.sum(lax.all_gather(frame_in, a_name), axis=0)  17 us
  transfers between devices with their start and end apart: 10, of which 7 were waited for; matrix products, arithmetic and copies ran while one was open for 8% of the time, Pallas kernels for 0%

profile of v1, /device:TPU:1, one launch (start us, length us, event | category | flops | bytes accessed | tf_op | source)
XLA Modules:
  0.0 427.2 jit_solution(18004346502139811795)
XLA Ops:
  7.4 2.7 copy.164
  10.1 10.0 %all-to-all-start.1 = ((bf16[3,8,2,128,128]{4,3,2,0,1:T(8,128)(2,1)}), bf16[3,8,2,128,128]{4,3,2,0,1:T(8,128)(2,1)S(1)}, u32[]{:S(2)}, u32[]{:S(2)}) async-start(bf16[3,8,2,128,128]{4,3,2,0,1:T(8,128)(2,1)} %copy.164), calls=%async_computation.1 | async-start | bytes 3145728 | tf_op jit(solution)/shard_map/all_to_all | solution.py:68
  20.1 33.3 %all-to-all-done.1 = bf16[3,8,2,128,128]{4,3,2,0,1:T(8,128)(2,1)S(1)} async-done(((bf16[3,8,2,128,128]{4,3,2,0,1:T(8,128)(2,1)}), bf16[3,8,2,128,128]{4,3,2,0,1:T(8,128)(2,1)S(1)}, u32[]{:S(2)}, u32[]{:S(2)}) %all-to-all-start.1) | async-done | bytes 1572896 | tf_op jit(solution)/shard_map/all_to_all | solution.py:68
  53.4 2.8 broadcast_select_fusion.3
  56.2 0.7 all-gather.15.cloned.1.call-update
  57.0 0.5 reduce-scatter.7.cloned.1.call-update
  57.6 0.5 reduce-scatter.5.cloned.1.call-update
  58.1 69.4 %all-gather.19.cloned.1.call-done = bf16[4,24,2,128,128]{4,3,2,1,0:T(8,128)(2,1)} async-done(((bf16[1,24,2,128,128]{4,3,2,1,0:T(8,128)(2,1)}), bf16[4,24,2,128,128]{4,3,2,1,0:T(8,128)(2,1)}) %all-gather.19.cloned.1.call-update) | async-done | bytes 6291472 | tf_op jit(solution)/shard_map/all_gather | solution.py:30
  127.6 5.7 %reduce_sum.102 = bf16[24,2,128,128]{3,2,1,0:T(8,128)(2,1)} reduce(bf16[4,24,2,128,128]{4,3,2,1,0:T(8,128)(2,1)} %all-gather.19.cloned.1.call-done, bf16[]{:T(256)} %constant.71.clone.1), dimensions={0}, to_apply=%region_12.13 | reduce | flops 2359296 | bytes 7864322 | tf_op jit(solution)/shard_map/reduce_sum | solution.py:30
  133.4 64.9 %all-gather.15.cloned.1.call-done = bf16[4,24,2,128,128]{4,3,2,1,0:T(8,128)(2,1)} async-done(((bf16[1,24,2,128,128]{4,3,2,1,0:T(8,128)(2,1)}), bf16[4,24,2,128,128]{4,3,2,1,0:T(8,128)(2,1)}) %all-gather.15.cloned.1.call-update) | async-done | bytes 6291472 | tf_op jit(solution)/shard_map/all_gather | solution.py:30
  198.3 5.7 %reduce_sum.98 = bf16[24,2,128,128]{3,2,1,0:T(8,128)(2,1)} reduce(bf16[4,24,2,128,128]{4,3,2,1,0:T(8,128)(2,1)} %all-gather.15.cloned.1.call-done, bf16[]{:T(256)} %constant.71.clone.1), dimensions={0}, to_apply=%region_4.5 | reduce | flops 2359296 | bytes 7864322 | tf_op jit(solution)/shard_map/reduce_sum | solution.py:30
  204.1 0.5 all-gather.21.cloned.1.call-update
  204.7 0.7 copy.151
  205.4 7.8 %all-to-all-start = ((s32[3,8,2]{0,2,1:T(2,128)}), s32[3,8,2]{0,2,1:T(2,128)S(1)}, u32[]{:S(2)}, u32[]{:S(2)}) async-start(s32[3,8,2]{0,2,1:T(2,128)} %copy.151), calls=%async_computation | async-start | bytes 16384 | tf_op jit(solution)/shard_map/all_to_all | solution.py:69
  213.2 0.6 dynamic-slice
  214.5 5.8 %all-to-all-done = s32[3,8,2]{0,2,1:T(2,128)S(1)} async-done(((s32[3,8,2]{0,2,1:T(2,128)}), s32[3,8,2]{0,2,1:T(2,128)S(1)}, u32[]{:S(2)}, u32[]{:S(2)}) %all-to-all-start) | async-done | bytes 224 | tf_op jit(solution)/shard_map/all_to_all | solution.py:69
  220.4 7.3 %all-reduce.2 = (s32[24,2]{0,1:T(2,128)S(1)}, s32[24,2]{0,1:T(2,128)S(1)}) all-reduce(s32[24,2]{0,1:T(2,128)S(1)} %get-tuple-element.28, s32[24,2]{0,1:T(2,128)S(1)} %get-tuple-element.27), channel_id=8, replica_groups=mesh['row_0'=4,'row_1'=2,'col'=8,'layer'=4] {'col'}, use_global_device_ids=true, to_apply=%region_10.11.clone | all-reduce | flops 96 | bytes 768
  227.7 14.1 %all-gather.5 = s32[8,3,2]{1,2,0:T(2,128)S(1)} all-gather(s32[1,3,2]{1,2,0:T(2,128)S(1)} %dynamic-slice_bitcast_fusion.1), channel_id=1, replica_groups=mesh['row_0'=4,'row_1'=2,'col'=8,'layer'=4] {'col'}, dimensions={0}, use_global_device_ids=true | all-gather | bytes 216 | tf_op jit(solution)/shard_map/all_gather | solution.py:22
  241.9 0.1 copy.156
  242.4 6.3 %all_gather.52 = s32[4,24,2]{1,2,0:T(2,128)S(1)} all-gather(s32[1,24,2]{1,2,0:T(2,128)S(1)} %select_n.168), channel_id=1, replica_groups=mesh['row_0'=4,'row_1'=2,'col'=8,'layer'=4] {'row_0'}, dimensions={0}, use_global_device_ids=true | all-gather | bytes 960 | tf_op jit(solution)/shard_map/all_gather | solution.py:30
  248.7 3.1 all-gather.4
  252.3 0.6 gather_fusion
  253.1 13.7 %all-gather.7 = s32[8,3,2]{1,2,0:T(2,128)S(1)} all-gather(s32[1,3,2]{1,2,0:T(2,128)S(1)} %dynamic-slice_bitcast_fusion), channel_id=1, replica_groups=mesh['row_0'=4,'row_1'=2,'col'=8,'layer'=4] {'col'}, dimensions={0}, use_global_device_ids=true | all-gather | bytes 216 | tf_op jit(solution)/shard_map/all_gather | solution.py:22
  266.8 0.1 copy.169
  267.2 5.8 %all_gather.60 = s32[4,24,2]{1,2,0:T(2,128)S(1)} all-gather(s32[1,24,2]{1,2,0:T(2,128)S(1)} %select_n.187), channel_id=1, replica_groups=mesh['row_0'=4,'row_1'=2,'col'=8,'layer'=4] {'row_0'}, dimensions={0}, use_global_device_ids=true | all-gather | bytes 960 | tf_op jit(solution)/shard_map/all_gather | solution.py:30
  273.0 3.6 all-gather.6
  277.1 0.6 gather_fusion.2
  277.8 0.6 iota_reduce_fusion
  278.5 0.1 copy.177
  278.6 0.1 reshape.133
  278.7 0.1 copy.176
  278.8 0.8 iota_reduce_fusion.1
  279.7 0.1 reshape.119
  279.9 0.1 copy.163
  280.0 2.8 reduce_sum.103
  282.8 20.6 %all-gather.23.cloned.1.call-done = bf16[48,2,128,128]{3,2,1,0:T(8,128)(2,1)} async-done(((bf16[24,2,128,128]{3,2,1,0:T(8,128)(2,1)}), bf16[48,2,128,128]{3,2,1,0:T(8,128)(2,1)}) %all-gather.23.cloned.1.call-update) | async-done | bytes 3145744 | tf_op jit(solution)/shard_map/all_gather | solution.py:30
  303.4 2.7 reduce_sum.99
  306.1 3.1 gather_fusion.3
  309.2 3.1 gather_fusion.1
  312.3 26.7 %all-gather.21.cloned.1.call-done = bf16[6144,128]{1,0:T(8,128)(2,1)} async-done(((bf16[768,128]{1,0:T(8,128)(2,1)}), bf16[6144,128]{1,0:T(8,128)(2,1)}) %all-gather.21.cloned.1.call-update) | async-done | bytes 1572880 | tf_op jit(solution)/shard_map/all_gather | solution.py:22
  339.1 4.8 %fusion.1 = f32[24,2,128,128,1]{2,3,1,4,0:T(8,128)} fusion(bf16[24,2,128,128,1]{3,2,4,1,0:T(8,128)(2,1)} %bitcast.128, bf16[24,2,2,128,128]{4,3,2,1,0:T(8,128)(2,1)} %bitcast.116, pred[24,2,2]{2,1,0:T(4,128)(4,1)S(1)} %copy.176), kind=kOutput, calls=%fused_computation.6 | convolution fusion | flops 404226048 | bytes 7864416 | tf_op jit(solution)/shard_map/iarc,iascd->isrd/dot_general | solution.py:60
  343.9 28.3 %all-gather.17.cloned.1.call-done = bf16[6144,128]{1,0:T(8,128)(2,1)} async-done(((bf16[768,128]{1,0:T(8,128)(2,1)}), bf16[6144,128]{1,0:T(8,128)(2,1)}) %all-gather.17.cloned.1.call-update) | async-done | bytes 1572880 | tf_op jit(solution)/shard_map/all_gather | solution.py:22
  372.1 3.0 fusion
  375.2 0.4 copy.195
  375.6 25.3 %all_to_all.47 = bf16[4,24,2,32,128]{4,3,2,1,0:T(8,128)(2,1)S(1)} all-to-all(bf16[4,24,2,32,128]{4,3,2,1,0:T(8,128)(2,1)S(1)} %bitcast.118), channel_id=1, replica_groups=mesh['row_0'=4,'row_1'=2,'col'=8,'layer'=4] {'layer'}, dimensions={0} | all-to-all | bytes 3145728 | tf_op jit(solution)/shard_map/all_to_all | solution.py:43
  400.9 0.3 reduce_sum.104
  401.2 17.7 %all_to_all.48 = bf16[24,1,2,32,128]{4,3,2,1,0:T(8,128)(2,1)S(1)} all-to-all(bf16[24,1,2,32,128]{4,3,2,1,0:T(8,128)(2,1)S(1)} %bitcast.127), channel_id=1, replica_groups=mesh['row_0'=4,'row_1'=2,'col'=8,'layer'=4] {'col'}, dimensions={0} | all-to-all | bytes 786432 | tf_op jit(solution)/shard_map/all_to_all | solution.py:99
  418.9 0.8 copy.180
  (65 shorter events, 2.8 us)
Async XLA Ops:
  10.1 43.3 %all-to-all-start.1 = ((bf16[3,8,2,128,128]{4,3,2,0,1:T(8,128)(2,1)}), bf16[3,8,2,128,128]{4,3,2,0,1:T(8,128)(2,1)S(1)}, u32[]{:S(2)}, u32[]{:S(2)}) async-start(bf16[3,8,2,128,128]{4,3,2,0,1:T(8,128)(2,1)} %copy.164), calls=%async_computation.1 | async-start | bytes 3145728 | tf_op jit(solution)/shard_map/all_to_all | solution.py:68
  20.1 107.5 %all-gather.19.cloned.1.call-start = ((), (), s32[]{:S(2)}) async-start(), calls=%async_computation.9 | async-start | bytes 7864320 | tf_op jit(solution)/shard_map/all_gather | solution.py:30
  56.2 142.1 %all-gather.15.cloned.1.call-start = ((), (), s32[]{:S(2)}) async-start(), calls=%async_computation.6 | async-start | bytes 7864320 | tf_op jit(solution)/shard_map/all_gather | solution.py:30
  56.9 147.2 %reduce-scatter.7.cloned.1.call-start = ((), (), s32[]{:S(2)}) async-start(), calls=%async_computation.10 | async-start | bytes 1769472 | tf_op jit(solution)/shard_map/reduce_scatter | solution.py:21
  57.5 194.8 %reduce-scatter.5.cloned.1.call-start = ((), (), s32[]{:S(2)}) async-start(), calls=%async_computation.7 | async-start | bytes 1769472 | tf_op jit(solution)/shard_map/reduce_scatter | solution.py:21
  58.1 221.9 %all-gather.25.cloned.1.call-start = ((), (), s32[]{:S(2)}) async-start(), calls=%async_computation.13 | async-start | bytes 4718592 | tf_op jit(solution)/shard_map/all_gather | solution.py:30
  133.3 170.0 %all-gather.23.cloned.1.call-start = ((), (), s32[]{:S(2)}) async-start(), calls=%async_computation.12 | async-start | bytes 4718592 | tf_op jit(solution)/shard_map/all_gather | solution.py:30
  204.0 0.7 copy-start.1
  204.0 9.2 %copy-start.2 = (u32[256]{0:T(256)S(1)}, u32[256]{0:T(256)}, u32[]{:S(2)}) copy-start(u32[256]{0:T(256)} %constant.104) | copy-start | bytes 3076
  204.0 135.0 %all-gather.21.cloned.1.call-start = ((), (), s32[]{:S(2)}) async-start(), calls=%async_computation.11 | async-start | bytes 1769472 | tf_op jit(solution)/shard_map/all_gather | solution.py:22
  205.4 14.9 %all-to-all-start = ((s32[3,8,2]{0,2,1:T(2,128)}), s32[3,8,2]{0,2,1:T(2,128)S(1)}, u32[]{:S(2)}, u32[]{:S(2)}) async-start(s32[3,8,2]{0,2,1:T(2,128)} %copy.151), calls=%async_computation | async-start | bytes 16384 | tf_op jit(solution)/shard_map/all_to_all | solution.py:69
  213.2 158.9 %all-gather.17.cloned.1.call-start = ((), (), s32[]{:S(2)}) async-start(), calls=%async_computation.8 | async-start | bytes 1769472 | tf_op jit(solution)/shard_map/all_gather | solution.py:22
  339.1 33.1 %copy-start = (bf16[96,128,128]{2,1,0:T(8,128)(2,1)S(1)}, bf16[96,128,128]{2,1,0:T(8,128)(2,1)}, u32[]{:S(2)}) copy-start(bf16[96,128,128]{2,1,0:T(8,128)(2,1)} %gather_fusion.1) | copy-start | bytes 9437188
Sparse Core Ops, SparseCore 0:
  56.3 71.2 all-gather.18
  129.4 68.8 all-gather.14
  200.1 51.0 all-gather.24
  252.9 50.4 all-gather.22
  305.0 33.9 all-gather.20
  340.7 31.3 all-gather.16
Sparse Core Ops, SparseCore 1:
  60.0 43.8 reduce-scatter.6
  106.3 40.2 reduce-scatter.4
